TPU v7x, 32 devices: a whole 2x2x4 slice. The times are simulated.
32 devices in a mesh: row: 4 (over x, core), col: 8 (over z, y).
Axes of the slice: x: 2, y: 2, z: 4, core: 2. Of those that a mesh axis runs over, the one named last changes fastest.
Arguments:
- ancestor_order: int32 [2, 48], replicated, may hold values from 0 to 47, each once within a row
- factor_rows: bfloat16 [2, 24576, 512], P(None, ('row', 'col')), may hold values from -0.0390625 to 0.0390625
- factor_inverse: bfloat16 [2, 512, 512], replicated
- ancestor_inverse: bfloat16 [24576, 24576], P('col', 'row'), may hold values from -6 to 6
- diagonal_inverse: float32 [2, 512, 512], P(None, None, 'row'), may hold values from -6 to 6
Outputs:
- offdiag_inverse: bfloat16 [2, 24576, 512], P(None, 'col', 'row')
- diag_updated: float32 [2, 512, 512], P(None, None, 'row')
Inputs may be any that keep to these rules, and one draw needn't show every extreme that they name: `ancestor_order`: each row lists every ancestor block once; its first 40 entries are the blocks coupled to that supernode.
All inputs are finite; a program needn't handle non-finite values.
Results may differ from a plain program's by a relative error of at most 0.011.
Values may be sent and summed in bfloat16 or wider, within the bound.
A program may use at most 128 MiB of HBM per device.

v0:
```python
import jax
import jax.numpy as jnp
from jax import lax
from jax.sharding import PartitionSpec as P

NSEL = 40


def broadcast(value, axis, source):
    kept = jnp.where(lax.axis_index(axis) == source, value, 0).astype(value.dtype)
    return lax.psum(kept, axis)


def process(listing, pieces, factor_inv, inverse_block, diag_inv):
    piece_rows = pieces.shape[1]
    block_width = pieces.shape[2]
    row_count = lax.axis_size("row")
    col_count = lax.axis_size("col")
    row_index = lax.axis_index("row")
    col_index = lax.axis_index("col")
    chosen = listing[:, :NSEL]
    first_row = (row_index * col_count + col_index) * piece_rows
    own_labels = (first_row + jnp.arange(piece_rows, dtype=jnp.int32)) // block_width
    own_keep = jnp.any(chosen[:, :, None] == own_labels[None, None, :], axis=1).astype(jnp.float32)
    normed = jnp.einsum("srk,skj->srj", pieces, factor_inv, preferred_element_type=jnp.float32)
    normed = (normed * own_keep[:, :, None]).astype(jnp.bfloat16)
    row_panel = lax.all_gather(normed, "col", axis=1, tiled=True)
    column_rows = inverse_block.shape[0]
    per_row = col_count // row_count
    offset = col_index % per_row * column_rows
    column_part = lax.dynamic_slice_in_dim(row_panel, offset, column_rows, 1)
    columns = broadcast(column_part, "row", col_index // per_row)
    partial_value = jnp.einsum(
        "pq,sqj->spj", inverse_block, row_panel, preferred_element_type=jnp.float32
    )
    lifted = columns.astype(jnp.float32)
    shares = lax.psum_scatter(partial_value, "row", scatter_dimension=2, tiled=True)
    local_terms = jnp.einsum("spk,spj->skj", lifted, shares, precision=lax.Precision.HIGHEST)
    correction = lax.psum(local_terms.astype(jnp.bfloat16), "col").astype(jnp.float32)
    col_labels = (col_index * column_rows + jnp.arange(column_rows, dtype=jnp.int32)) // block_width
    col_keep = jnp.any(chosen[:, :, None] == col_labels[None, None, :], axis=1).astype(jnp.float32)
    offdiag = (-(shares * col_keep[:, :, None])).astype(jnp.bfloat16)
    return (offdiag, diag_inv + correction)


def body(ancestor_order, factor_rows, factor_inverse, ancestor_inverse, diagonal_inverse):
    return process(ancestor_order, factor_rows, factor_inverse, ancestor_inverse, diagonal_inverse)


def solution(mesh):
    placed = (P(), P(None, ("row", "col"), None), P(), P("col", "row"), P(None, None, "row"))
    return jax.shard_map(
        body,
        mesh=mesh,
        in_specs=placed,
        out_specs=(P(None, "col", "row"), P(None, None, "row")),
        check_vma=False,
    )
```

profile of v0, /device:TPU:1, one launch (start us, length us, event | category | flops | bytes accessed | tf_op | source)
XLA Modules:
  0.0 505.2 jit_solution(1334670819939079602)
XLA Ops:
  7.2 0.0 copy-start
  7.2 0.0 all-gather.2.cloned.1.call-start
  7.3 0.9 compare_reduce_fusion.1
  8.2 0.4 copy-done
  8.6 3.3 multiply_convert_fusion
  11.9 0.0 all-gather.2.cloned.1.call-update
  12.0 0.0 all-reduce.3.cloned.1.call-start
  12.0 177.5 %all-gather.2.cloned.1.call-done = bf16[2,6144,512]{2,1,0:T(8,128)(2,1)} async-done(((bf16[2,768,512]{2,1,0:T(8,128)(2,1)}), bf16[2,6144,512]{2,1,0:T(8,128)(2,1)}) %all-gather.2.cloned.1.call-update) | async-done | bytes 12582928 | tf_op jit(solution)/shard_map/all_gather | solution.py:27
  189.6 6.6 %dynamic-slice_select_fusion = bf16[2,3072,512]{2,1,0:T(8,128)(2,1)} fusion(bf16[2,6144,512]{2,1,0:T(8,128)(2,1)} %all-gather.2.cloned.1.call-done, s32[]{:T(128)S(6)} %select_n.45, pred[]{:T(512)S(6)} %eq.37), kind=kLoop, calls=%fused_computation.3 | loop fusion | flops 3145728 | bytes 12582917 | tf_op jit(solution)/shard_map/jit(_where)/select_n | solution.py:10
  196.2 0.0 all-reduce.3.cloned.1.call-update
  196.2 0.0 reduce-scatter.2.cloned.1.call-start
  196.2 49.2 %fusion.2 = f32[2,3072,512]{1,2,0:T(8,128)} fusion(bf16[2,6144,512]{2,1,0:T(8,128)(2,1)} %all-gather.2.cloned.1.call-done, bf16[3072,6144]{1,0:T(8,128)(2,1)} %param.8), kind=kOutput, calls=%fused_computation.2 | convolution fusion | flops 38654705664 | bytes 62914560 | tf_op jit(solution)/shard_map/pq,sqj->spj/dot_general | solution.py:33
  245.5 0.0 copy-start.2
  245.5 0.0 reduce-scatter.2.cloned.1.call-update
  245.5 0.2 all-reduce.5.cloned.1.call-start
  245.8 0.4 copy-done.2
  246.2 0.2 compare_reduce_fusion
  246.4 68.0 %all-reduce.3.cloned.1.call-done = bf16[2,3072,512]{2,1,0:T(8,128)(2,1)} async-done(((bf16[2,3072,512]{2,1,0:T(8,128)(2,1)}), bf16[2,3072,512]{2,1,0:T(8,128)(2,1)}) %all-reduce.3.cloned.1.call-update) | async-done | bytes 6291472 | tf_op jit(solution)/shard_map/psum | solution.py:11
  314.4 102.7 %reduce-scatter.2.cloned.1.call-done = f32[2,3072,128]{1,2,0:T(8,128)} async-done(((f32[2,3072,512]{1,2,0:T(8,128)}), f32[2,3072,128]{1,2,0:T(8,128)}) %reduce-scatter.2.cloned.1.call-update) | async-done | bytes 3145744 | tf_op jit(solution)/shard_map/reduce_scatter | solution.py:37
  417.1 10.1 %convolution_convert_fusion = bf16[2,512,128]{2,1,0:T(8,128)(2,1)} fusion(bf16[2,3072,512]{2,1,0:T(8,128)(2,1)} %all-reduce.3.cloned.1.call-done, f32[2,3072,128]{1,2,0:T(8,128)} %reduce-scatter.2.cloned.1.call-done), kind=kOutput, calls=%fused_computation.6 | convolution fusion | flops 4831969280 | bytes 9699328 | tf_op jit(solution)/shard_map/spk,spj->skj/dot_general | solution.py:38
  427.1 0.0 all-reduce.5.cloned.1.call-update
  427.2 0.0 copy-start.1
  427.2 2.3 negate_convert_fusion
  429.5 1.6 copy.14
  431.1 65.6 %all-reduce.5.cloned.1.call-done = bf16[2,512,128]{2,1,0:T(8,128)(2,1)} async-done(((bf16[2,512,128]{2,1,0:T(8,128)(2,1)}), bf16[2,512,128]{2,1,0:T(8,128)(2,1)}) %all-reduce.5.cloned.1.call-update) | async-done | bytes 262160 | tf_op jit(solution)/shard_map/psum | solution.py:39
  496.7 1.9 convert_add_fusion
  498.6 0.0 copy-done.1
  (4 shorter events, 0.0 us)
Async XLA Ops:
  7.2 1.4 copy-start
  7.2 182.4 %all-gather.2.cloned.1.call-start = ((), (), s32[]{:S(2)}) async-start(), calls=%async_computation.1 | async-start | bytes 14155776 | tf_op jit(solution)/shard_map/all_gather | solution.py:27
  12.0 302.4 %all-reduce.3.cloned.1.call-start = ((), (), s32[]{:S(2)}) async-start(), calls=%async_computation.3 | async-start | bytes 12582912 | tf_op jit(solution)/shard_map/psum | solution.py:11
  196.2 220.9 %reduce-scatter.2.cloned.1.call-start = ((), (), s32[]{:S(2)}) async-start(), calls=%async_computation.2 | async-start | bytes 15728640 | tf_op jit(solution)/shard_map/reduce_scatter | solution.py:37
  245.5 0.7 copy-start.2
  245.5 251.2 %all-reduce.5.cloned.1.call-start = ((), (), s32[]{:S(2)}) async-start(), calls=%async_computation.4 | async-start | bytes 524288 | tf_op jit(solution)/shard_map/psum | solution.py:39
  427.2 71.4 %copy-start.1 = (bf16[2,768,512]{2,1,0:T(8,128)(2,1)S(1)}, bf16[2,768,512]{2,1,0:T(8,128)(2,1)}, u32[]{:S(2)}) copy-start(bf16[2,768,512]{2,1,0:T(8,128)(2,1)} %param.6) | copy-start | bytes 4718596
Sparse Core Ops, SparseCore 0:
  12.1 177.4 all-gather.1
  196.3 118.0 all-reduce.2
  317.0 100.0 reduce-scatter.1
  427.3 69.3 all-reduce.4
where the time goes:
time: 508 us; the launch traced here: 505 us
  waiting for transfers between devices  414 us (81%)
  matrix products  62.6 us (12%)
  between operations  13.9 us (3%)
  other arithmetic  12 us (2%)
    all_gather x1, waiting for transfers between devices, process(): row_panel = lax.all_gather(normed, 'col', axis=1, tiled=True)  178 us
    reduce_scatter x1, waiting for transfers between devices, process(): lax.psum_scatter(partial_value, 'row', scatter_dimension=2, tiled=True)  103 us
    psum x1, waiting for transfers between devices, broadcast(): return lax.psum(kept, axis)  68 us
    psum x1, waiting for transfers between devices, process(): lax.psum(local_terms.astype(jnp.bfloat16), 'col').astype(jnp.float32)  65.6 us
    dot_general x1, matrix products, process(): jnp.einsum('pq,sqj->spj', inverse_block, row_panel, preferred_element_typ...  49.2 us
  transfers between devices with their start and end apart: 4, of which 4 were waited for; matrix products, arithmetic and copies ran while one was open for 11% of the time, Pallas kernels for 0%

commit v1 on v0

v1 whole, which is shorter than its diff:
```python
import functools

import jax
import jax.numpy as jnp
from jax import lax
from jax.experimental import pallas as pl
from jax.experimental.pallas import tpu as pltpu
from jax.sharding import PartitionSpec as P

NSEL = 40
MESH = pl.DeviceIdType.MESH


def kernel(
    dims, strips, own_ref, a_ref, out_ref, corr_ref,
    panel, abuf, acc, s1, r1, s2, r2, kept, below, cs, cr, total,
    own_sem, a_sem, ring_s, ring_r, s1s, r1s, s2s, r2s, bel_s, bel_r, bel_l, cs_s, cs_r, ag_s, ag_r,
):
    chips, n, depth = dims
    supers = own_ref.shape[0] // 2
    chunks = own_ref.shape[0]
    piece, wide = own_ref.shape[1], own_ref.shape[2]
    rows = acc.shape[1]
    width = wide // chips
    half = piece // 2
    tall = rows // 4
    per_slab = rows // piece
    slabs = n // per_slab
    r = lax.axis_index("row")
    c = lax.axis_index("col")
    x, k = r // 2, r % 2
    mate = x * 2 + 1 - k
    source_row = c // slabs
    source_x, source_k = source_row // 2, source_row % 2
    length = n // depth

    def col_at(pos):
        y, i = pos // length, pos % length
        return (i + (y % 2) * (length - 1 - 2 * i)) * depth + y

    y, z = c % depth, c // depth
    pos = y * length + z + (y % 2) * (length - 1 - 2 * z)
    right, left = col_at((pos + 1) % n), col_at((pos + n - 1) % n)

    def a_copy(i):
        src = place(i)[4]
        if strips:
            view = a_ref.at[src]
        else:
            view = a_ref.at[:, pl.ds(pl.multiple_of(src * piece, piece), piece)]
        return pltpu.make_async_copy(view, abuf.at[i % 2], a_sem.at[i % 2])

    def place(i):
        g, j = i // n, i % n
        t = (j + 1) // 2
        last = j // (n - 1)
        d = last * (g % 2) + (1 - last) * (1 - j % 2)
        return g, j, t, d, col_at((pos + (2 * d - 1) * t + n) % n)

    def ring(g, t, d, h, src):
        view = panel.at[g, src, pl.ds(h * half, half)]
        return pltpu.make_async_remote_copy(
            src_ref=view, dst_ref=view,
            send_sem=ring_s.at[d, g, t - 1, h], recv_sem=ring_r.at[d, g, t - 1, h],
            device_id=(r, right * (1 - d) + left * d), device_id_type=MESH,
        )

    def send_own(g):
        for h in range(2):
            for d in range(2):
                ring(g, 1, d, h, c).start()

    def below_copy(g, src, i, to_row, sem):
        return pltpu.make_async_remote_copy(
            src_ref=src, dst_ref=below.at[g, i], send_sem=sem, recv_sem=bel_r.at[g, i],
            device_id=(to_row, c), device_id_type=MESH,
        )

    def first_copy(s, b):
        return pltpu.make_async_remote_copy(
            src_ref=s1.at[s, b], dst_ref=r1.at[s, b], send_sem=s1s.at[s, b], recv_sem=r1s.at[s, b],
            device_id=(mate, c), device_id_type=MESH,
        )

    def second_copy(s, b, slot):
        return pltpu.make_async_remote_copy(
            src_ref=s2.at[s, b], dst_ref=r2.at[s, slot], send_sem=s2s.at[s, b], recv_sem=r2s.at[s, slot],
            device_id=(b * 2 + k, c), device_id_type=MESH,
        )

    def stage1(g):
        s = g // 2

        @pl.when(k != g % 2)
        def _():
            for b in range(chips):
                @pl.loop(0, 4)
                def _(m):
                    at = pl.ds(pl.multiple_of(m * tall, tall), tall)
                    s1[s, b, at, :] = acc[g % 2, at, pl.ds(b * width, width)].astype(jnp.bfloat16)
                first_copy(s, b).start()

    def stage2(g):
        s = g // 2

        @pl.when(k == g % 2)
        def _():
            for b in range(chips):
                first_copy(s, b).wait_recv()

                @pl.when(x == b)
                def _():
                    @pl.loop(0, 4)
                    def _(m):
                        at = pl.ds(pl.multiple_of(m * tall, tall), tall)
                        kept[s, at, :] = acc[g % 2, at, pl.ds(b * width, width)] + r1[s, b, at, :].astype(jnp.float32)

                @pl.when(x != b)
                def _():
                    @pl.loop(0, 4)
                    def _(m):
                        at = pl.ds(pl.multiple_of(m * tall, tall), tall)
                        both = acc[g % 2, at, pl.ds(b * width, width)] + r1[s, b, at, :].astype(jnp.float32)
                        s2[s, b, at, :] = both.astype(jnp.bfloat16)
                    second_copy(s, b, x).start()

    def stage3(g):
        s = g // 2

        @pl.when(k == g % 2)
        def _():
            for b in range(chips):
                @pl.when(x != b)
                def _():
                    second_copy(s, b, b).wait_recv()

                    @pl.loop(0, 4)
                    def _(m):
                        at = pl.ds(pl.multiple_of(m * tall, tall), tall)
                        kept[s, at, :] += r2[s, b, at, :].astype(jnp.float32)

            @pl.loop(0, 4)
            def _(m):
                at = pl.ds(pl.multiple_of(m * tall, tall), tall)
                out_ref[s, at, :] = kept[s, at, :].astype(jnp.bfloat16)

    def pass_below(g):
        @pl.when((k == source_k) & (x != source_x))
        def _():
            for i in range(per_slab):
                below_copy(g, below.at[g, i], i, mate, bel_s.at[g, i, chips]).wait_recv()
                below_copy(g, below.at[g, i], i, mate, bel_s.at[g, i, chips]).start()

    def local_own(g):
        return pltpu.make_async_copy(own_ref.at[g], panel.at[g, c], own_sem.at[g])

    for g in range(chunks):
        local_own(g).start()
    a_copy(0).start()
    barrier = pltpu.get_barrier_semaphore()
    for delta in range(1, n):
        pl.semaphore_signal(barrier, inc=1, device_id=(r, (c + delta) % n), device_id_type=MESH)
    pl.semaphore_signal(barrier, inc=1, device_id=(mate, c), device_id_type=MESH)
    for delta in range(1, chips):
        pl.semaphore_signal(barrier, inc=1, device_id=(((x + delta) % chips) * 2 + k, c), device_id_type=MESH)
    pl.semaphore_wait(barrier, n - 1 + 1 + chips - 1)
    for g in range(chunks):
        local_own(g).wait()
    send_own(0)

    @pl.loop(0, chunks * n)
    def _(i):
        g, j, t, d, src = place(i)

        @pl.when(j >= 1)
        def _():
            for h in range(2):
                ring(g, t, d, h, src).wait_recv()

                @pl.when((t + 1 < n // 2) | ((t + 1 == n // 2) & (d == g % 2)))
                def _():
                    ring(g, t + 1, d, h, src).start()

        @pl.when((j == n - 2) & (g < chunks - 1))
        def _():
            send_own(g + 1)

        @pl.when((r == source_row) & (src // per_slab == c % slabs))
        def _():
            at = src % per_slab
            for delta in range(1, chips):
                to = ((x + delta) % chips) * 2 + k
                below_copy(g, panel.at[g, src], at, to, bel_s.at[g, at, delta]).start()
            below_copy(g, panel.at[g, src], at, mate, bel_s.at[g, at, chips]).start()
            pltpu.make_async_copy(panel.at[g, src], below.at[g, at], bel_l.at[g, at]).start()

        a_copy(i).wait()

        @pl.when(i + 1 < chunks * n)
        def _():
            a_copy(i + 1).start()

        slot = i % 2

        @pl.loop(0, 4)
        def _(m):
            at = pl.ds(pl.multiple_of(m * tall, tall), tall)
            term = jnp.dot(abuf[slot, at, :], panel[g, src], preferred_element_type=jnp.float32)

            @pl.when(j == 0)
            def _():
                acc[g % 2, at, :] = term

            @pl.when(j > 0)
            def _():
                acc[g % 2, at, :] += term

        @pl.when(j == n - 1)
        def _():
            stage1(g)

        @pl.when((j == 1) & (g > 0))
        def _():
            stage2(g - 1)

        @pl.when((j == 3) & (g > 0))
        def _():
            pass_below(g - 1)

        @pl.when((j == n - 3) & (g > 0))
        def _():
            stage3(g - 1)

    stage2(chunks - 1)
    pass_below(chunks - 1)

    @pl.loop(0, chunks)
    def _(g):
        for i in range(per_slab):
            @pl.when(r == source_row)
            def _():
                pltpu.make_async_copy(panel.at[g, c], below.at[g, i], bel_l.at[g, i]).wait()

            @pl.when(k != source_k)
            def _():
                below_copy(g, below.at[g, i], i, mate, bel_s.at[g, i, chips]).wait_recv()

    stage3(chunks - 1)

    part = width // n

    @pl.loop(0, chunks)
    def _(g):
        term = jnp.zeros((width, wide), jnp.float32)
        for i in range(per_slab):
            term += lax.dot_general(
                out_ref[g // 2, pl.ds(i * piece, piece), :], below[g, i],
                (((0,), (0,)), ((), ())), preferred_element_type=jnp.float32,
            )
        for b in range(n):
            cs[b, g] = term[b * part:(b + 1) * part, :].astype(jnp.bfloat16)

    def scatter(delta):
        to = (c + delta) % n
        return pltpu.make_async_remote_copy(
            src_ref=cs.at[to], dst_ref=cr.at[delta], send_sem=cs_s.at[delta], recv_sem=cs_r.at[delta],
            device_id=(r, to), device_id_type=MESH,
        )

    def gather(delta, slot):
        return pltpu.make_async_remote_copy(
            src_ref=total, dst_ref=corr_ref.at[slot], send_sem=ag_s.at[delta], recv_sem=ag_r.at[delta],
            device_id=(r, (c + delta) % n), device_id_type=MESH,
        )

    for delta in range(1, n):
        scatter(delta).start()
    summed = cs[c].astype(jnp.float32)
    for delta in range(1, n):
        scatter(delta).wait_recv()
        summed += cr[delta].astype(jnp.float32)
    total[...] = summed.astype(jnp.bfloat16)
    for delta in range(1, n):
        gather(delta, c).start()
    corr_ref[c] = total[...]
    for delta in range(1, n):
        gather(delta, (c + n - delta) % n).wait_recv()

    for delta in range(1, n):
        scatter(delta).wait_send()
        gather(delta, c).wait_send()

    @pl.loop(0, chunks)
    def _(g):
        @pl.loop(1, n // 2 + 1)
        def _(t):
            for d in range(2):
                @pl.when((t < n // 2) | (d == g % 2))
                def _():
                    for h in range(2):
                        ring(g, t, d, h, c).wait_send()

        for i in range(per_slab):
            @pl.when(r == source_row)
            def _():
                for delta in range(1, chips):
                    below_copy(g, panel.at[g, c], i, mate, bel_s.at[g, i, delta]).wait_send()
                below_copy(g, panel.at[g, c], i, mate, bel_s.at[g, i, chips]).wait_send()

            @pl.when((k == source_k) & (x != source_x))
            def _():
                below_copy(g, below.at[g, i], i, mate, bel_s.at[g, i, chips]).wait_send()

    for s in range(supers):
        for b in range(chips):
            first_copy(s, b).wait_send()

            @pl.when(x != b)
            def _():
                second_copy(s, b, x).wait_send()


def body(ancestor_order, factor_rows, factor_inverse, ancestor_inverse, diagonal_inverse):
    supers, piece, block = factor_rows.shape
    rows = ancestor_inverse.shape[0]
    row_count, n = lax.axis_size("row"), lax.axis_size("col")
    r, c = lax.axis_index("row"), lax.axis_index("col")
    chips = row_count // 2
    depth = chips
    width = block // row_count
    wide = chips * width
    chunks = supers * 2
    chosen = ancestor_order[:, :NSEL]

    own_labels = ((r * n + c) * piece + jnp.arange(piece, dtype=jnp.int32)) // block
    own_keep = jnp.any(chosen[:, :, None] == own_labels[None, None, :], axis=1).astype(jnp.float32)
    inverse = factor_inverse.reshape(supers, block, chips, 2, width).transpose(0, 3, 1, 2, 4)
    inverse = inverse.reshape(supers, 2, block, wide)
    normed = jnp.einsum("srk,spkj->sprj", factor_rows, inverse, preferred_element_type=jnp.float32)
    normed = (normed * own_keep[:, None, :, None]).astype(jnp.bfloat16).reshape(chunks, piece, wide)

    strips = piece % 128 != 0
    left = ancestor_inverse
    if strips:
        left = left.reshape(rows, n, piece).transpose(1, 0, 2)
    per_slab = rows // piece
    part = width // n
    half_type, full_type, dma = jnp.bfloat16, jnp.float32, pltpu.SemaphoreType.DMA
    product, correction = pl.pallas_call(
        functools.partial(kernel, (chips, n, depth), strips),
        out_shape=(
            jax.ShapeDtypeStruct((supers, rows, width), half_type),
            jax.ShapeDtypeStruct((n, chunks, part, wide), half_type),
        ),
        in_specs=[pl.BlockSpec(memory_space=pl.ANY)] * 2,
        out_specs=(pl.BlockSpec(memory_space=pltpu.VMEM),) * 2,
        scratch_shapes=[
            pltpu.VMEM((chunks, n, piece, wide), half_type),
            pltpu.VMEM((2, rows, piece), half_type),
            pltpu.VMEM((2, rows, wide), full_type),
            pltpu.VMEM((supers, chips, rows, width), half_type),
            pltpu.VMEM((supers, chips, rows, width), half_type),
            pltpu.VMEM((supers, chips, rows, width), half_type),
            pltpu.VMEM((supers, chips, rows, width), half_type),
            pltpu.VMEM((supers, rows, width), full_type),
            pltpu.VMEM((chunks, per_slab, piece, wide), half_type),
            pltpu.VMEM((n, chunks, part, wide), half_type),
            pltpu.VMEM((n, chunks, part, wide), half_type),
            pltpu.VMEM((chunks, part, wide), half_type),
            dma((chunks,)),
            dma((2,)),
            dma((2, chunks, n // 2, 2)),
            dma((2, chunks, n // 2, 2)),
            dma((supers, chips)),
            dma((supers, chips)),
            dma((supers, chips)),
            dma((supers, chips)),
            dma((chunks, per_slab, chips + 1)),
            dma((chunks, per_slab)),
            dma((chunks, per_slab)),
            dma((n,)),
            dma((n,)),
            dma((n,)),
            dma((n,)),
        ],
        compiler_params=pltpu.CompilerParams(
            collective_id=0, has_side_effects=True, vmem_limit_bytes=64 * 1024 * 1024 - 65536
        ),
        cost_estimate=pl.CostEstimate(
            flops=2 * rows * n * piece * supers * block, bytes_accessed=8 * rows * n * piece, transcendentals=0
        ),
    )(normed, left)

    labels = (c * rows + jnp.arange(rows, dtype=jnp.int32)) // block
    keep = jnp.any(chosen[:, :, None] == labels[None, None, :], axis=1).astype(jnp.float32)
    offdiag = (-(product.astype(jnp.float32) * keep[:, :, None])).astype(jnp.bfloat16)
    correction = correction.astype(jnp.float32).reshape(n, supers, 2, part, chips, width)
    correction = correction.transpose(1, 4, 2, 5, 0, 3).reshape(supers, block, width)
    return offdiag, diagonal_inverse + correction


def solution(mesh):
    placed = (P(), P(None, ("row", "col"), None), P(), P("col", "row"), P(None, None, "row"))
    return jax.shard_map(
        body,
        mesh=mesh,
        in_specs=placed,
        out_specs=(P(None, "col", "row"), P(None, None, "row")),
        check_vma=False,
    )
```

time: 508 us -> 193 us (0.38)
  waiting for transfers between devices: 414 us -> 0 us
  Pallas kernels: 0 us -> 178 us
  matrix products: 62.6 us -> 2.42 us
  between operations: 13.9 us -> 0.77 us
  other arithmetic: 12 us -> 4.82 us
    pallas_call x0 -> x1, Pallas kernels: none -> 178 us  [body(): pl.pallas_call(functools.partial(kernel, (chips, n, depth), strips), out_...]
    all_gather x1 -> x0, waiting for transfers between devices: 178 us -> none  [process(): row_panel = lax.all_gather(normed, 'col', axis=1, tiled=True)]
    psum x2 -> x0, waiting for transfers between devices: 134 us -> none  [the longest x1 68 us: broadcast(): return lax.psum(kept, axis)]
    reduce_scatter x1 -> x0, waiting for transfers between devices: 103 us -> none  [process(): lax.psum_scatter(partial_value, 'row', scatter_dimension=2, tiled=True)]
    dot_general x3 -> x1, matrix products: 62.6 us -> 2.42 us  [body(): jnp.einsum('srk,spkj->sprj', factor_rows, inverse, preferred_element_type...]
    select_n x3 -> x2, other arithmetic: 6.61 us -> 0.02 us  [the longest x1 0.01 us: body(): labels = (c * rows + jnp.arange(rows, dtype=jnp.int32)) // block]
  transfers between devices with their start and end apart: 4 -> 0, of which waited for: 4 -> 0; matrix products, arithmetic and copies ran while one was open for 11% -> 0% of each run, Pallas kernels for 0% -> 0%
where the time goes in v1:
time: 193 us; the launch traced here: 192 us
  Pallas kernels  178 us (92%)
  local copies, waits for them, and re-layouts  6.66 us (3%)
  other arithmetic  4.82 us (2%)
  matrix products  2.42 us (1%)
    pallas_call x1, Pallas kernels, body(): pl.pallas_call(functools.partial(kernel, (chips, n, depth), strips), out_...  178 us

profile of v1, /device:TPU:1, one launch (start us, length us, event | category | flops | bytes accessed | tf_op | source)
XLA Modules:
  0.0 192.4 jit_solution(15142636329973924850)
XLA Ops:
  0.7 0.8 compare_reduce_fusion.1
  1.5 1.3 reshape.68
  2.8 1.5 copy.15
  4.3 2.4 %fusion.1 = bf16[2,2,768,256]{2,3,1,0:T(8,128)(2,1)S(1)} fusion(f32[2,768]{1,0:T(2,128)S(1)} %convert_element_type.27, bf16[2,2,512,256]{2,3,1,0:T(8,128)(2,1)S(1)} %bitcast.24, bf16[2,768,512]{2,1,0:T(8,128)(2,1)} %param.6), kind=kOutput, calls=%fused_computation.3 | convolution fusion | flops 806879232 | bytes 4200448 | tf_op jit(solution)/shard_map/srk,spkj->sprj/dot_general | solution.py:339
  6.7 1.6 copy.16
  8.3 177.7 %shard_map.68 = (bf16[2,3072,128]{2,1,0:T(8,128)(2,1)}, bf16[8,4,16,256]{3,2,1,0:T(8,128)(2,1)}) custom-call(bf16[4,768,256]{2,1,0:T(8,128)(2,1)} %bitcast.23, bf16[3072,6144]{1,0:T(8,128)(2,1)} %a_ref.1), custom_call_target="tpu_custom_call" | custom-call | flops 38654705664 | bytes 150994944 | tf_op jit(solution)/shard_map/pallas_call | solution.py:349
  186.0 0.9 compare_reduce_fusion
  186.9 0.0 copy-start.1
  187.0 3.0 %negate_convert_fusion = bf16[2,3072,128]{2,1,0:T(8,128)(2,1)} fusion(bf16[2,3072,128]{2,1,0:T(8,128)(2,1)} %get-tuple-element.4, f32[2,3072]{1,0:T(2,128)S(1)} %convert_element_type.31), kind=kLoop, calls=%fused_computation | loop fusion | flops 3145728 | bytes 3170304 | tf_op jit(solution)/shard_map/convert_element_type | solution.py:396
  190.0 0.0 copy-start
  190.0 0.0 copy-done.1
  190.0 0.3 reshape.78
  190.3 0.4 copy.22
  190.7 0.4 reshape.75
  191.1 0.0 copy-done
  191.1 0.2 copy.18
  191.3 0.1 add.41
  191.4 1.0 copy.19
  (4 shorter events, 0.0 us)
Async XLA Ops:
  186.9 3.1 %copy-start.1 = (bf16[8,4,16,256]{3,2,1,0:T(8,128)(2,1)S(1)}, bf16[8,4,16,256]{3,2,1,0:T(8,128)(2,1)}, u32[]{:S(2)}) copy-start(bf16[8,4,16,256]{3,2,1,0:T(8,128)(2,1)} %get-tuple-element.5) | copy-start | bytes 786436
  190.0 1.1 copy-start

commit v2 on v1

v2 whole, which is shorter than its diff:
```python
import functools

import jax
import jax.numpy as jnp
from jax import lax
from jax.experimental import pallas as pl
from jax.experimental.pallas import tpu as pltpu
from jax.sharding import PartitionSpec as P

NSEL = 40
MESH = pl.DeviceIdType.MESH


def kernel(
    dims, strips, order_ref, factor_ref, inverse_ref, a_ref, out_ref, corr_ref,
    panel, abuf, acc, s1, r1, s2, r2, kept, below, cs, cr, total,
    a_sem, ring_s, ring_r, s1s, r1s, s2s, r2s, bel_s, bel_r, bel_l, cs_s, cs_r, ag_s, ag_r,
):
    chips, n, depth = dims
    supers, piece, block = factor_ref.shape
    chunks = supers * 2
    rows, wide = acc.shape[1], acc.shape[2]
    width = wide // chips
    half = piece // 2
    tall = rows // 4
    per_slab = rows // piece
    slabs = n // per_slab
    r = lax.axis_index("row")
    c = lax.axis_index("col")
    x, k = r // 2, r % 2
    mate = x * 2 + 1 - k
    source_row = c // slabs
    source_x, source_k = source_row // 2, source_row % 2
    length = n // depth

    def col_at(pos):
        y, i = pos // length, pos % length
        return (i + (y % 2) * (length - 1 - 2 * i)) * depth + y

    y, z = c % depth, c // depth
    pos = y * length + z + (y % 2) * (length - 1 - 2 * z)
    right, left = col_at((pos + 1) % n), col_at((pos + n - 1) % n)

    def a_copy(i):
        src = place(i)[4]
        if strips:
            view = a_ref.at[src]
        else:
            view = a_ref.at[:, pl.ds(pl.multiple_of(src * piece, piece), piece)]
        return pltpu.make_async_copy(view, abuf.at[i % 2], a_sem.at[i % 2])

    def place(i):
        g, j = i // n, i % n
        t = (j + 1) // 2
        last = j // (n - 1)
        d = last * (g % 2) + (1 - last) * (1 - j % 2)
        return g, j, t, d, col_at((pos + (2 * d - 1) * t + n) % n)

    def ring(g, t, d, h, src):
        view = panel.at[g, src, pl.ds(h * half, half)]
        return pltpu.make_async_remote_copy(
            src_ref=view, dst_ref=view,
            send_sem=ring_s.at[d, g, t - 1, h], recv_sem=ring_r.at[d, g, t - 1, h],
            device_id=(r, right * (1 - d) + left * d), device_id_type=MESH,
        )

    def coupled(s, first, count):
        low = order_ref[pl.ds(s, 1), 0:NSEL] * block
        label = first + lax.broadcasted_iota(jnp.int32, (count, NSEL), 0)
        return jnp.sum(jnp.where((label >= low) & (label < low + block), 1.0, 0.0), axis=1, keepdims=True)

    def norm(g):
        s, p = g // 2, g % 2
        keep = coupled(s, (r * n + c) * piece, piece)
        for b in range(chips):
            at = pl.ds((2 * b + p) * width, width)
            term = jnp.dot(factor_ref[s], inverse_ref[s, :, at], preferred_element_type=jnp.float32)
            panel[g, c, :, pl.ds(b * width, width)] = (term * keep).astype(jnp.bfloat16)

    def below_copy(g, src, i, to_row, sem):
        return pltpu.make_async_remote_copy(
            src_ref=src, dst_ref=below.at[g, i], send_sem=sem, recv_sem=bel_r.at[g, i],
            device_id=(to_row, c), device_id_type=MESH,
        )

    def tile(m):
        return pl.ds(pl.multiple_of(m * tall, tall), tall)

    def first_copy(s, b, m):
        return pltpu.make_async_remote_copy(
            src_ref=s1.at[s, b, tile(m)], dst_ref=r1.at[s, b, tile(m)],
            send_sem=s1s.at[s, b, m], recv_sem=r1s.at[s, b, m],
            device_id=(mate, c), device_id_type=MESH,
        )

    def second_copy(s, b, m, slot):
        return pltpu.make_async_remote_copy(
            src_ref=s2.at[s, b, tile(m)], dst_ref=r2.at[s, slot, tile(m)],
            send_sem=s2s.at[s, b, m], recv_sem=r2s.at[s, slot, m],
            device_id=(b * 2 + k, c), device_id_type=MESH,
        )

    def stage1(g, m):
        s = g // 2
        for b in range(chips):
            s1[s, b, tile(m), :] = acc[g % 2, tile(m), pl.ds(b * width, width)].astype(jnp.bfloat16)
            first_copy(s, b, m).start()

    def stage2(g):
        s = g // 2

        @pl.when(k == g % 2)
        def _():
            @pl.loop(0, 4)
            def _(m):
                for b in range(chips):
                    first_copy(s, b, m).wait_recv()
                    both = acc[g % 2, tile(m), pl.ds(b * width, width)] + r1[s, b, tile(m), :].astype(jnp.float32)

                    @pl.when(x == b)
                    def _():
                        kept[s, tile(m), :] = both

                    @pl.when(x != b)
                    def _():
                        s2[s, b, tile(m), :] = both.astype(jnp.bfloat16)
                        second_copy(s, b, m, x).start()

    def stage3(g):
        s = g // 2

        @pl.when(k == g % 2)
        def _():
            @pl.loop(0, 4)
            def _(m):
                for b in range(chips):
                    @pl.when(x != b)
                    def _():
                        second_copy(s, b, m, b).wait_recv()
                        kept[s, tile(m), :] += r2[s, b, tile(m), :].astype(jnp.float32)
                keep = coupled(s, c * rows + m * tall, tall)
                out_ref[s, tile(m), :] = (-(kept[s, tile(m), :] * keep)).astype(jnp.bfloat16)

    def pass_below(g):
        @pl.when((k == source_k) & (x != source_x))
        def _():
            for i in range(per_slab):
                below_copy(g, below.at[g, i], i, mate, bel_s.at[g, i, chips]).wait_recv()
                below_copy(g, below.at[g, i], i, mate, bel_s.at[g, i, chips]).start()

    def scatter(s, delta):
        to = (c + delta) % n
        return pltpu.make_async_remote_copy(
            src_ref=cs.at[s, to], dst_ref=cr.at[s, delta],
            send_sem=cs_s.at[s, delta], recv_sem=cs_r.at[s, delta],
            device_id=(r, to), device_id_type=MESH,
        )

    def gather(s, delta, slot):
        return pltpu.make_async_remote_copy(
            src_ref=total.at[s], dst_ref=corr_ref.at[s, slot],
            send_sem=ag_s.at[s, delta], recv_sem=ag_r.at[s, delta],
            device_id=(r, (c + delta) % n), device_id_type=MESH,
        )

    def wait_below(s):
        for q in range(2):
            for i in range(per_slab):
                g = 2 * s + q

                @pl.when(r == source_row)
                def _():
                    pltpu.make_async_copy(panel.at[g, c], below.at[g, i], bel_l.at[g, i]).wait()

                @pl.when(k != source_k)
                def _():
                    below_copy(g, below.at[g, i], i, mate, bel_s.at[g, i, chips]).wait_recv()

    def correct(s):
        for q in range(2):
            term = jnp.zeros((width, wide), jnp.float32)
            for i in range(per_slab):
                term -= lax.dot_general(
                    out_ref[s, pl.ds(i * piece, piece), :], below[2 * s + q, i],
                    (((0,), (0,)), ((), ())), preferred_element_type=jnp.float32,
                )
            for b in range(n):
                cs[s, b, q] = term[b * part:(b + 1) * part, :].astype(jnp.bfloat16)
        for delta in range(1, n):
            scatter(s, delta).start()

    def collect(s):
        summed = cs[s, c].astype(jnp.float32)
        for delta in range(1, n):
            scatter(s, delta).wait_recv()
            summed += cr[s, delta].astype(jnp.float32)
        total[s] = summed.astype(jnp.bfloat16)
        for delta in range(1, n):
            gather(s, delta, c).start()
        corr_ref[s, c] = summed.astype(jnp.bfloat16)

    part = width // n
    barrier = pltpu.get_barrier_semaphore()
    for delta in range(1, n):
        pl.semaphore_signal(barrier, inc=1, device_id=(r, (c + delta) % n), device_id_type=MESH)
    pl.semaphore_signal(barrier, inc=1, device_id=(mate, c), device_id_type=MESH)
    for delta in range(1, chips):
        pl.semaphore_signal(barrier, inc=1, device_id=(((x + delta) % chips) * 2 + k, c), device_id_type=MESH)
    a_copy(0).start()
    norm(0)
    pl.semaphore_wait(barrier, n - 1 + 1 + chips - 1)
    for h in range(2):
        for d in range(2):
            ring(0, 1, d, h, c).start()
    for g in range(1, chunks):
        norm(g)

    @pl.loop(0, chunks * n)
    def _(i):
        g, j, t, d, src = place(i)

        ahead, h = j // 2 + 1, j % 2
        for way in range(2):
            @pl.when((ahead < n // 2) | (way == g % 2))
            def _():
                come = col_at((pos + (2 * way - 1) * ahead + n) % n)
                ring(g, ahead, way, h, come).wait_recv()

                @pl.when((ahead + 1 < n // 2) | ((ahead + 1 == n // 2) & (way == g % 2)))
                def _():
                    ring(g, ahead + 1, way, h, come).start()

            @pl.when((g < chunks - 1) & (j == n - 5 + 2 * ((g + way + 1) % 2)))
            def _():
                for first in range(2):
                    ring(g + 1, 1, way, first, c).start()

        @pl.when((r == source_row) & (src // per_slab == c % slabs))
        def _():
            at = src % per_slab
            for delta in range(1, chips):
                to = ((x + delta) % chips) * 2 + k
                below_copy(g, panel.at[g, src], at, to, bel_s.at[g, at, delta]).start()
            below_copy(g, panel.at[g, src], at, mate, bel_s.at[g, at, chips]).start()
            pltpu.make_async_copy(panel.at[g, src], below.at[g, at], bel_l.at[g, at]).start()

        a_copy(i).wait()

        @pl.when(i + 1 < chunks * n)
        def _():
            a_copy(i + 1).start()

        slot = i % 2

        @pl.loop(0, 4)
        def _(m):
            at = pl.ds(pl.multiple_of(m * tall, tall), tall)
            term = jnp.dot(abuf[slot, at, :], panel[g, src], preferred_element_type=jnp.float32)

            @pl.when(j == 0)
            def _():
                acc[g % 2, at, :] = term

            @pl.when(j > 0)
            def _():
                acc[g % 2, at, :] += term

            @pl.when((j == n - 1) & (k != g % 2))
            def _():
                stage1(g, m)

        @pl.when((j == 1) & (g > 0))
        def _():
            stage2(g - 1)

        @pl.when((j == 3) & (g > 0))
        def _():
            pass_below(g - 1)

        @pl.when((j == n - 3) & (g > 0))
        def _():
            stage3(g - 1)

        @pl.when((j == 2) & (g >= 3) & (g % 2 == 1))
        def _():
            wait_below((g - 3) // 2)
            correct((g - 3) // 2)

        @pl.when((j == n - 2) & (g >= 3) & (g % 2 == 1))
        def _():
            collect((g - 3) // 2)

    stage2(chunks - 1)
    pass_below(chunks - 1)
    wait_below(supers - 1)
    stage3(chunks - 1)
    correct(supers - 1)
    collect(supers - 1)
    for s in range(supers):
        for delta in range(1, n):
            gather(s, delta, (c + n - delta) % n).wait_recv()
            scatter(s, delta).wait_send()
            gather(s, delta, c).wait_send()

    @pl.loop(0, chunks)
    def _(g):
        @pl.loop(1, n // 2 + 1)
        def _(t):
            for d in range(2):
                @pl.when((t < n // 2) | (d == g % 2))
                def _():
                    for h in range(2):
                        ring(g, t, d, h, c).wait_send()

        for i in range(per_slab):
            @pl.when(r == source_row)
            def _():
                for delta in range(1, chips):
                    below_copy(g, panel.at[g, c], i, mate, bel_s.at[g, i, delta]).wait_send()
                below_copy(g, panel.at[g, c], i, mate, bel_s.at[g, i, chips]).wait_send()

            @pl.when((k == source_k) & (x != source_x))
            def _():
                below_copy(g, below.at[g, i], i, mate, bel_s.at[g, i, chips]).wait_send()

    for s in range(supers):
        for b in range(chips):
            @pl.loop(0, 4)
            def _(m):
                first_copy(s, b, m).wait_send()

                @pl.when(x != b)
                def _():
                    second_copy(s, b, m, x).wait_send()


def body(ancestor_order, factor_rows, factor_inverse, ancestor_inverse, diagonal_inverse):
    supers, piece, block = factor_rows.shape
    rows = ancestor_inverse.shape[0]
    row_count, n = lax.axis_size("row"), lax.axis_size("col")
    chips = row_count // 2
    depth = chips
    width = block // row_count
    wide = chips * width
    chunks = supers * 2

    strips = piece % 128 != 0
    left = ancestor_inverse
    if strips:
        left = left.reshape(rows, n, piece).transpose(1, 0, 2)
    per_slab = rows // piece
    part = width // n
    half_type, full_type, dma = jnp.bfloat16, jnp.float32, pltpu.SemaphoreType.DMA
    offdiag, correction = pl.pallas_call(
        functools.partial(kernel, (chips, n, depth), strips),
        out_shape=(
            jax.ShapeDtypeStruct((supers, rows, width), half_type),
            jax.ShapeDtypeStruct((supers, n, 2, part, wide), half_type),
        ),
        in_specs=[pl.BlockSpec(memory_space=pltpu.VMEM)] * 3 + [pl.BlockSpec(memory_space=pl.ANY)],
        out_specs=(pl.BlockSpec(memory_space=pltpu.VMEM),) * 2,
        scratch_shapes=[
            pltpu.VMEM((chunks, n, piece, wide), half_type),
            pltpu.VMEM((2, rows, piece), half_type),
            pltpu.VMEM((2, rows, wide), full_type),
            pltpu.VMEM((supers, chips, rows, width), half_type),
            pltpu.VMEM((supers, chips, rows, width), half_type),
            pltpu.VMEM((supers, chips, rows, width), half_type),
            pltpu.VMEM((supers, chips, rows, width), half_type),
            pltpu.VMEM((supers, rows, width), full_type),
            pltpu.VMEM((chunks, per_slab, piece, wide), half_type),
            pltpu.VMEM((supers, n, 2, part, wide), half_type),
            pltpu.VMEM((supers, n, 2, part, wide), half_type),
            pltpu.VMEM((supers, 2, part, wide), half_type),
            dma((2,)),
            dma((2, chunks, n // 2, 2)),
            dma((2, chunks, n // 2, 2)),
            dma((supers, chips, 4)),
            dma((supers, chips, 4)),
            dma((supers, chips, 4)),
            dma((supers, chips, 4)),
            dma((chunks, per_slab, chips + 1)),
            dma((chunks, per_slab)),
            dma((chunks, per_slab)),
            dma((supers, n)),
            dma((supers, n)),
            dma((supers, n)),
            dma((supers, n)),
        ],
        compiler_params=pltpu.CompilerParams(
            collective_id=0, has_side_effects=True, vmem_limit_bytes=64 * 1024 * 1024 - 65536
        ),
        cost_estimate=pl.CostEstimate(
            flops=2 * rows * n * piece * supers * block, bytes_accessed=8 * rows * n * piece, transcendentals=0
        ),
    )(ancestor_order, factor_rows, factor_inverse, left)

    correction = correction.astype(jnp.float32).reshape(supers, n, 2, part, chips, width)
    correction = correction.transpose(0, 4, 2, 5, 1, 3).reshape(supers, block, width)
    return offdiag, diagonal_inverse + correction


def solution(mesh):
    placed = (P(), P(None, ("row", "col"), None), P(), P("col", "row"), P(None, None, "row"))
    return jax.shard_map(
        body,
        mesh=mesh,
        in_specs=placed,
        out_specs=(P(None, "col", "row"), P(None, None, "row")),
        check_vma=False,
    )
```

time: 193 us -> 173 us (0.90)
  Pallas kernels: 178 us -> 166 us
  other arithmetic: 4.82 us -> 0.08 us
  matrix products: 2.42 us -> 0 us
    pallas_call x1, Pallas kernels: 178 us -> 166 us  [body(): pl.pallas_call(functools.partial(kernel, (chips, n, depth), strips), out_...]
    convert_element_type x3 -> x0, other arithmetic: 3.06 us -> none  [the longest x1 3.04 us: body(): (-(product.astype(jnp.float32) * keep[:, :, None])).astype(jnp.bfloat16)]
    unnamed x6 -> x5, local copies, waits for them, and re-layouts: 1.2 us -> 3.88 us
    dot_general x1 -> x0, matrix products: 2.42 us -> none  [body(): jnp.einsum('srk,spkj->sprj', factor_rows, inverse, preferred_element_type...]
where the time goes in v2:
time: 173 us; the launch traced here: 172 us
  Pallas kernels  166 us (96%)
  local copies, waits for them, and re-layouts  5.92 us (3%)
    pallas_call x1, Pallas kernels, body(): pl.pallas_call(functools.partial(kernel, (chips, n, depth), strips), out_...  166 us
    unnamed x5, local copies, waits for them, and re-layouts  3.88 us

profile of v2, /device:TPU:1, one launch (start us, length us, event | category | flops | bytes accessed | tf_op | source)
XLA Modules:
  0.0 172.4 jit_solution(1857424111416595412)
XLA Ops:
  0.6 165.8 %shard_map.68 = (bf16[2,3072,128]{2,1,0:T(8,128)(2,1)}, bf16[2,8,2,16,256]{4,3,2,1,0:T(8,128)(2,1)}) custom-call(s32[2,48]{1,0:T(2,128)} %order_ref.1, bf16[2,768,512]{2,1,0:T(8,128)(2,1)} %factor_ref.1, bf16[2,512,512]{2,1,0:T(8,128)(2,1)} %inverse_ref.1, bf16[3072,6144]{1,0:T(8,128)(2,1)} %a_ref.1), custom_call_target="tpu_custom_call" | custom-call | flops 38654705664 | bytes 150994944 | tf_op jit(solution)/shard_map/pallas_call | solution.py:354
  166.4 1.2 copy.9
  167.6 1.2 reshape.21
  168.8 0.4 copy.12
  169.3 0.4 reshape.18
  169.7 0.0 copy-start
  169.7 0.1 add.3
  169.8 1.0 copy.10
  170.8 0.5 copy-done
  171.3 1.1 copy.14
Async XLA Ops:
  169.7 1.6 copy-start
